TPU v7x, 32 devices: a whole 2x2x4 slice. The times are simulated.
32 devices in a mesh: kpt: 2 (over x), row: 8 (over z, y), col: 2 (over core).
Axes of the slice: x: 2, y: 2, z: 4, core: 2. Of those that a mesh axis runs over, the one named last changes fastest.
Arguments:
- wannier: float32 [64, 32, 1024], P('kpt', ('row', 'col')), parts along dimension 0, may hold values from -6 to 6
- pairs: int32 [384, 2], replicated, may hold values from 0 to 31, as said below
- gmap: int32 [8192], replicated, may hold values from 1 to 32767, as said below
- screened: bfloat16 [4, 2, 8192, 8192], P('kpt', None, 'row', 'col'), parts along dimension 0, may hold values from -0.046875 to 0.046875
Outputs:
- coulomb: float32 [2, 2, 768, 384], P(None, None, ('kpt', 'row', 'col')), parts along dimension 2
There are 2 independent parts, one for each index of `kpt`. A program takes and returns all parts, laid end to end along the dimension named above; an argument that names none is the same for every part. Nothing has to cross between parts.
Inputs may be any that keep to these rules, and one draw needn't show every extreme that they name: `gmap`: 8192 distinct flat cells of the grid; cell 0 is never among them. `pairs`: in each row the first Wannier function is no greater than the second; no two rows are equal.
All inputs are finite; a program needn't handle non-finite values.
Results may differ from a plain program's by a relative error of at most 0.0082.
Values may be sent and summed in bfloat16 or wider, within the bound.
No kernel may reach another device: no remote copies, remote signals or barrier semaphores. Data moves between devices by JAX's collectives and lax.ppermute only.
A program may use at most 128 MiB of HBM per device.

v0:
```python
import math
import jax
import jax.numpy as jnp
from jax import lax
from jax.sharding import PartitionSpec as P

NW = 32
GX = 32
NG = 8192
NP = 384


def line_tables(side_len):
    positions = jnp.arange(side_len, dtype=jnp.int32)
    phase_index = positions[:, None] * positions[None, :] % side_len
    angles = phase_index.astype(jnp.float32) * (2.0 * math.pi / side_len)
    return (jnp.cos(angles), jnp.sin(angles))


def plane_transform(density):
    cosine, sine_table = line_tables(GX)
    highest = lax.Precision.HIGHEST
    shaped = density.reshape(-1, GX, GX)
    real_z = jnp.einsum("nyz,kz->nyk", shaped, cosine, precision=highest)
    imag_z = -jnp.einsum("nyz,kz->nyk", shaped, sine_table, precision=highest)
    new_real = jnp.einsum("jy,nyk->njk", cosine, real_z, precision=highest) + jnp.einsum(
        "jy,nyk->njk", sine_table, imag_z, precision=highest
    )
    new_imag = jnp.einsum("jy,nyk->njk", cosine, imag_z, precision=highest) - jnp.einsum(
        "jy,nyk->njk", sine_table, real_z, precision=highest
    )
    return (new_real.reshape(density.shape), new_imag.reshape(density.shape))


def line_transform(real_part, imag_part):
    cosine, sine_table = line_tables(GX)
    highest = lax.Precision.HIGHEST
    new_real = jnp.einsum("kn,pny->pky", cosine, real_part, precision=highest) + jnp.einsum(
        "kn,pny->pky", sine_table, imag_part, precision=highest
    )
    new_imag = jnp.einsum("kn,pny->pky", cosine, imag_part, precision=highest) - jnp.einsum(
        "kn,pny->pky", sine_table, real_part, precision=highest
    )
    return (new_real, new_imag)


def right_columns(screened, segment):
    w_real = screened[:, 0]
    w_imag = screened[:, 1]
    real_real = jnp.einsum("fgh,bh->fgb", w_real, segment[0], preferred_element_type=jnp.float32)
    imag_imag = jnp.einsum("fgh,bh->fgb", w_imag, segment[1], preferred_element_type=jnp.float32)
    real_imag = jnp.einsum("fgh,bh->fgb", w_real, segment[1], preferred_element_type=jnp.float32)
    imag_real = jnp.einsum("fgh,bh->fgb", w_imag, segment[0], preferred_element_type=jnp.float32)
    return jnp.stack([real_real - imag_imag, real_imag + imag_real], axis=1)


def shards(wannier, pairs, gmap, screened):
    planes = wannier.shape[1]
    grid_cells = wannier.shape[2]
    members = jnp.arange(NW, dtype=jnp.int32)[None, :]
    pick_first = (pairs[:, 0:1] == members).astype(jnp.float32)
    pick_second = (pairs[:, 1:2] == members).astype(jnp.float32)
    flat_rows = wannier.reshape(NW, -1)
    highest = lax.Precision.HIGHEST
    density = jnp.dot(pick_first, flat_rows, precision=highest) * jnp.dot(
        pick_second, flat_rows, precision=highest
    )
    density = density.reshape(NP, planes, grid_cells)
    arrived = lax.all_to_all(density, ("row", "col"), split_axis=0, concat_axis=1, tiled=True)
    real_part, imag_part = plane_transform(arrived)
    real_part, imag_part = line_transform(real_part, imag_part)
    owned = real_part.shape[0]
    norm_factor = 1.0 / math.sqrt(GX * GX * GX)
    rho_real = jnp.take(real_part.reshape(owned, -1), gmap, axis=1) * norm_factor
    rho_imag = jnp.take(imag_part.reshape(owned, -1), gmap, axis=1) * norm_factor
    rho = jnp.stack([rho_real, rho_imag], axis=0).astype(jnp.bfloat16)
    row_span = screened.shape[2]
    halves = lax.all_to_all(rho, "col", split_axis=2, concat_axis=1, tiled=True)
    screened_rho = right_columns(screened, lax.all_gather(halves, "row", axis=1, tiled=True))
    blocks = lax.all_to_all(rho, "row", split_axis=2, concat_axis=1, tiled=True)
    blocks = blocks.reshape(2, lax.axis_size("row"), owned, row_span)
    left_panel = lax.all_gather(blocks, "col", axis=2, tiled=True).reshape(2, NP, row_span)
    left_wide = left_panel.astype(jnp.float32)
    u_real = jnp.einsum(
        "ag,fgb->fab", left_wide[0], screened_rho[:, 0], precision=highest
    ) + jnp.einsum("ag,fgb->fab", left_wide[1], screened_rho[:, 1], precision=highest)
    u_imag = jnp.einsum(
        "ag,fgb->fab", left_wide[0], screened_rho[:, 1], precision=highest
    ) - jnp.einsum("ag,fgb->fab", left_wide[1], screened_rho[:, 0], precision=highest)
    partial_terms = jnp.stack([u_real, u_imag], axis=1) / math.sqrt(NG)
    summed = lax.psum(partial_terms, ("row", "col"))
    share_rows = NP // lax.axis_size(("row", "col"))
    return lax.dynamic_slice_in_dim(
        summed, lax.axis_index(("row", "col")) * share_rows, share_rows, 2
    )


def solution(mesh):
    return jax.shard_map(
        shards,
        mesh=mesh,
        in_specs=(P("kpt", ("row", "col"), None), P(), P(), P("kpt", None, "row", "col")),
        out_specs=P(None, None, ("kpt", "row", "col"), None),
        check_vma=False,
    )
```

profile of v0, /device:TPU:0, one launch (start us, length us, event | category | flops | bytes accessed | tf_op | source)
XLA Modules:
  0.0 687.3 jit_solution(8600309741713015094)
XLA Ops:
  11.3 3.8 reshape.35
  15.1 7.5 %all-to-all-start = ((f32[384,2,1024]{2,1,0:T(2,128)}), f32[384,2,1024]{2,1,0:T(2,128)S(1)}, u32[]{:S(2)}, u32[]{:S(2)}) async-start(f32[384,2,1024]{2,1,0:T(2,128)} %reshape.35), calls=%async_computation | async-start | bytes 6291456 | tf_op jit(solution)/shard_map/all_to_all | solution.py:69
  22.7 59.1 %all-to-all-done = f32[384,2,1024]{2,1,0:T(2,128)S(1)} async-done(((f32[384,2,1024]{2,1,0:T(2,128)}), f32[384,2,1024]{2,1,0:T(2,128)S(1)}, u32[]{:S(2)}, u32[]{:S(2)}) %all-to-all-start) | async-done | bytes 3145760 | tf_op jit(solution)/shard_map/all_to_all | solution.py:69
  82.9 2.4 copy.71
  85.3 7.6 %reshape.36 = f32[768,32,32]{2,1,0:T(8,128)} reshape(f32[24,16,2,1024]{3,2,1,0:T(2,128)S(1)} %copy.71) | data formatting | bytes 6291456 | tf_op jit(solution)/shard_map/reshape | solution.py:23
  92.9 9.2 %copy.72 = f32[768,32,32]{0,2,1:T(8,128)S(1)} copy(f32[768,32,32]{2,1,0:T(8,128)} %reshape.36) | data formatting | bytes 6291456 | tf_op jit(solution)/shard_map/reshape | solution.py:23
  102.1 3.0 convolution_negate_fusion
  105.1 3.0 fusion.72
  108.1 4.9 fusion.22
  113.1 5.2 fusion.24
  118.2 6.7 add_bitcast_fusion.1
  125.0 5.5 subtract_bitcast_fusion.1
  130.5 10.6 %copy.79 = f32[768,32,32]{2,1,0:T(8,128)} copy(f32[768,32,32]{0,1,2:T(8,128)S(1)} %subtract_bitcast_fusion.1) | data formatting | bytes 6291456 | tf_op jit(solution)/shard_map/sub | solution.py:29
  141.1 9.4 %reshape.38 = f32[24,32,1024]{2,1,0:T(8,128)S(1)} reshape(f32[768,32,32]{2,1,0:T(8,128)} %copy.79) | data formatting | bytes 6291456 | tf_op jit(solution)/shard_map/reshape | solution.py:32
  150.4 5.5 fusion.66
  155.9 11.4 %copy.76 = f32[768,32,32]{2,1,0:T(8,128)} copy(f32[768,32,32]{0,1,2:T(8,128)} %add_bitcast_fusion.1) | data formatting | bytes 6291456 | tf_op jit(solution)/shard_map/add | solution.py:26
  167.3 10.7 %reshape.37 = f32[24,32,1024]{2,1,0:T(8,128)} reshape(f32[768,32,32]{2,1,0:T(8,128)} %copy.76) | data formatting | bytes 6291456 | tf_op jit(solution)/shard_map/reshape | solution.py:32
  178.0 5.9 fusion.69
  184.0 5.5 subtract_bitcast_fusion
  189.5 5.6 add_bitcast_fusion
  195.1 10.3 %copy.89 = f32[24,32,1024]{0,2,1:T(8,128)} copy(f32[24,32,1024]{2,1,0:T(8,128)} %add_bitcast_fusion) | data formatting | bytes 6291456 | tf_op jit(solution)/shard_map/reshape | solution.py:74
  205.4 8.6 %copy.90 = f32[24,32,1024]{0,2,1:T(8,128)} copy(f32[24,32,1024]{2,1,0:T(8,128)S(1)} %copy-done.2) | data formatting | bytes 6291456 | tf_op jit(solution)/shard_map/reshape | solution.py:75
  214.0 33.6 %gather_fusion = f32[8192,24]{1,0:T(8,128)} fusion(f32[24,32768]{0,1:T(8,128)} %bitcast.144, s32[8192]{0:T(1024)S(1)} %fusion.57), kind=kCustom, calls=%fused_computation.clone | custom fusion | bytes 1605632 | tf_op jit(solution)/shard_map/jit(_take)/gather | solution.py:74
  247.6 33.6 %gather_fusion.1 = f32[8192,24]{1,0:T(8,128)} fusion(f32[24,32768]{0,1:T(8,128)} %bitcast.143, s32[8192]{0:T(1024)S(1)} %fusion.57), kind=kCustom, calls=%fused_computation.1.clone | custom fusion | bytes 1605632 | tf_op jit(solution)/shard_map/jit(_take)/gather | solution.py:75
  281.3 7.2 %fusion.30 = (bf16[1,24,8192]{1,2,0:T(8,128)(2,1)S(1)}, bf16[1,24,8192]{1,2,0:T(8,128)(2,1)S(1)}) fusion(f32[8192,24]{1,0:T(8,128)} %gather_fusion, pred[8192]{0:T(1024)(128)(4,1)S(1)} %compare_and_fusion, f32[8192,24]{1,0:T(8,128)} %gather_fusion.1), kind=kLoop, calls=%fused_computation.43 | loop fusion | flops 1179648 | bytes 2367488 | tf_op jit(solution)/shard_map/stack | solution.py:76
  289.4 35.5 %copy.108 = bf16[2,24,8192]{1,0,2:T(2,128)(2,1)} copy(bf16[2,24,8192]{1,2,0:T(8,128)(2,1)S(1)} %pad_maximum_fusion) | data formatting | bytes 1572864 | tf_op jit(solution)/shard_map/stack | solution.py:76
  324.9 6.6 reshape.71
  331.5 35.8 %all_to_all.48 = bf16[8,2,24576]{2,1,0:T(2,128)(2,1)S(1)} all-to-all(bf16[8,2,24576]{2,1,0:T(2,128)(2,1)S(1)} %reshape.71), channel_id=1, replica_groups=mesh['kpt'=2,'row'=8,'col'=2] {'row'}, dimensions={0} | all-to-all | bytes 1572864 | tf_op jit(solution)/shard_map/all_to_all | solution.py:80
  367.3 6.9 %reshape.72 = bf16[8192,2,24]{2,1,0:T(2,128)(2,1)} reshape(bf16[8,2,24576]{2,1,0:T(2,128)(2,1)S(1)} %all_to_all.48) | data formatting | bytes 1572864
  374.3 10.3 %copy.87 = bf16[2,24,8,1024]{3,1,2,0:T(8,128)(2,1)} copy(bf16[2,24,8,1024]{1,0,3,2:T(2,128)(2,1)} %bitcast.145) | data formatting | bytes 1572864 | tf_op jit(solution)/shard_map/all_to_all | solution.py:80
  384.6 10.2 %copy.109 = bf16[2,24,8192]{1,0,2:T(2,128)(2,1)} copy(bf16[2,24,8192]{1,2,0:T(8,128)(2,1)} %copy-done) | data formatting | bytes 1572864 | tf_op jit(solution)/shard_map/stack | solution.py:76
  394.8 7.0 %reshape.73 = bf16[2,2,98304]{2,1,0:T(2,128)(2,1)S(1)} reshape(bf16[8192,2,24]{2,1,0:T(2,128)(2,1)} %bitcast.147) | data formatting | bytes 1572864
  401.9 4.4 all_to_all.49
  406.2 7.3 %reshape.74 = bf16[8192,2,24]{2,1,0:T(2,128)(2,1)} reshape(bf16[2,2,98304]{2,1,0:T(2,128)(2,1)S(1)} %all_to_all.49) | data formatting | bytes 1572864
  413.6 9.5 %copy.83 = bf16[2,24,2,4096]{3,1,2,0:T(8,128)(2,1)} copy(bf16[2,24,2,4096]{1,0,3,2:T(2,128)(2,1)} %bitcast.146) | data formatting | bytes 1572864 | tf_op jit(solution)/shard_map/all_to_all | solution.py:78
  423.1 1.5 fusion.129
  424.7 96.3 %all-gather.3.cloned.1.call-done = bf16[2,384,4096]{2,1,0:T(8,128)(2,1)} async-done(((bf16[2,48,4096]{2,1,0:T(8,128)(2,1)}), bf16[2,384,4096]{2,1,0:T(8,128)(2,1)}) %all-gather.3.cloned.1.call-update) | async-done | bytes 6291472 | tf_op jit(solution)/shard_map/all_gather | solution.py:79
  521.0 11.4 %fusion = f32[384,2,1024]{2,0,1:T(8,128)S(1)} fusion(bf16[2,2,1024,4096]{3,2,1,0:T(8,128)(2,1)} %param.9, bf16[2,384,4096]{2,1,0:T(8,128)(2,1)} %all-gather.3.cloned.1.call-done), kind=kOutput, calls=%fused_computation.2 | convolution fusion | flops 6442450944 | bytes 23068672 | tf_op jit(solution)/shard_map/fgh,bh->fgb/dot_general | solution.py:53
  532.4 11.2 %fusion.39 = f32[384,2,1024]{2,0,1:T(8,128)S(1)} fusion(f32[384,2,1024]{2,0,1:T(8,128)S(1)} %fusion, bf16[2,2,1024,4096]{3,2,1,0:T(8,128)(2,1)} %param.9, bf16[2,384,4096]{2,1,0:T(8,128)(2,1)} %all-gather.3.cloned.1.call-done), kind=kOutput, calls=%fused_computation.47 | convolution fusion | flops 6443237376 | bytes 26214400 | tf_op jit(solution)/shard_map/fgh,bh->fgb/dot_general | solution.py:52
  543.6 2.6 fusion.14
  546.2 2.6 fusion.16
  548.9 12.6 %fusion.2 = f32[384,2,1024]{2,0,1:T(8,128)} fusion(bf16[2,2,1024,4096]{3,2,1,0:T(8,128)(2,1)} %param.9, bf16[2,384,4096]{2,1,0:T(8,128)(2,1)} %all-gather.3.cloned.1.call-done), kind=kOutput, calls=%fused_computation.4 | convolution fusion | flops 6442450944 | bytes 23068672 | tf_op jit(solution)/shard_map/fgh,bh->fgb/dot_general | solution.py:51
  561.5 12.1 %fusion.36 = f32[384,2,1024]{2,0,1:T(8,128)S(1)} fusion(f32[384,2,1024]{2,0,1:T(8,128)} %fusion.2, bf16[2,2,1024,4096]{3,2,1,0:T(8,128)(2,1)} %param.9, bf16[2,384,4096]{2,1,0:T(8,128)(2,1)} %all-gather.3.cloned.1.call-done), kind=kOutput, calls=%fused_computation.46 | convolution fusion | flops 6443237376 | bytes 26214400 | tf_op jit(solution)/shard_map/fgh,bh->fgb/dot_general | solution.py:50
  573.6 2.7 fusion.48
  576.3 2.7 fusion.51
  579.0 1.6 maximum_multiply_fusion
  580.6 97.4 %all-reduce.2.cloned.1.call-done = f32[2,2,384,384]{2,3,0,1:T(8,128)} async-done(((f32[2,2,384,384]{2,3,0,1:T(8,128)}), f32[2,2,384,384]{2,3,0,1:T(8,128)}) %all-reduce.2.cloned.1.call-update) | async-done | bytes 2359312 | tf_op jit(solution)/shard_map/psum | solution.py:91
  678.0 1.7 constant_dynamic-slice_fusion
  (26 shorter events, 7.9 us)
Async XLA Ops:
  15.1 7.6 %copy-start.4 = (s32[8192]{0:T(1024)S(1)}, s32[8192]{0:T(1024)}, u32[]{:S(2)}) copy-start(s32[8192]{0:T(1024)} %param.8) | copy-start | bytes 98308
  15.1 66.8 %all-to-all-start = ((f32[384,2,1024]{2,1,0:T(2,128)}), f32[384,2,1024]{2,1,0:T(2,128)S(1)}, u32[]{:S(2)}, u32[]{:S(2)}) async-start(f32[384,2,1024]{2,1,0:T(2,128)} %reshape.35), calls=%async_computation | async-start | bytes 6291456 | tf_op jit(solution)/shard_map/all_to_all | solution.py:69
  22.6 400.5 %all-gather.5.cloned.1.call-start = ((), (), s32[]{:S(2)}) async-start(), calls=%async_computation.4 | async-start | bytes 2359296 | tf_op jit(solution)/shard_map/all_gather | solution.py:82
  178.0 6.0 copy-start.1
  178.0 6.0 copy-start.3
  195.1 10.3 %copy-start.2 = (f32[24,32,1024]{2,1,0:T(8,128)S(1)}, f32[24,32,1024]{2,1,0:T(8,128)}, u32[]{:S(2)}) copy-start(f32[24,32,1024]{2,1,0:T(8,128)} %subtract_bitcast_fusion) | copy-start | bytes 9437188
  289.4 35.5 %copy-start = (bf16[2,24,8192]{1,2,0:T(8,128)(2,1)}, bf16[2,24,8192]{1,2,0:T(8,128)(2,1)S(1)}, u32[]{:S(2)}) copy-start(bf16[2,24,8192]{1,2,0:T(8,128)(2,1)S(1)} %pad_maximum_fusion) | copy-start | bytes 2359300
  384.6 136.4 %all-gather.3.cloned.1.call-start = ((), (), s32[]{:S(2)}) async-start(), calls=%async_computation.3 | async-start | bytes 7077888 | tf_op jit(solution)/shard_map/all_gather | solution.py:79
  423.1 254.9 %all-reduce.2.cloned.1.call-start = ((), (), s32[]{:S(2)}) async-start(), calls=%async_computation.5 | async-start | bytes 4718592 | tf_op jit(solution)/shard_map/psum | solution.py:91
Sparse Core Ops, SparseCore 0:
  384.7 8.8 all-gather.4
  423.2 97.7 all-gather.2
  580.7 97.1 all-reduce.1
where the time goes:
time: 696 us; the launch traced here: 687 us
  waiting for transfers between devices  253 us (36%)
  local copies, waits for them, and re-layouts  251 us (36%)
  matrix products  112 us (16%)
  blocking collectives  40.2 us (6%)
  between operations  13.7 us (2%)
  other arithmetic  9.75 us (1%)
  starting transfers between devices  7.67 us (1%)
    psum x1, waiting for transfers between devices, shards(): summed = lax.psum(partial_terms, ('row', 'col'))  97.4 us
    all_gather x1, waiting for transfers between devices, shards(): lax.all_gather(halves, 'row', axis=1, tiled=True)  96.3 us
    all_to_all x1, waiting for transfers between devices, shards(): lax.all_to_all(density, ('row', 'col'), split_axis=0, concat_axis=1, tile...  59.1 us
    another operation x2, local copies, waits for them, and re-layouts, shards(): rho = jnp.stack([rho_real, rho_imag], axis=0).astype(jnp.bfloat16)  45.7 us
    all_to_all x1, blocking collectives, shards(): blocks = lax.all_to_all(rho, 'row', split_axis=2, concat_axis=1, tiled=True)  35.8 us
    gather x1, local copies, waits for them, and re-layouts, shards(): jnp.take(imag_part.reshape(owned, -1), gmap, axis=1) * norm_factor  33.6 us
    gather x1, local copies, waits for them, and re-layouts, shards(): jnp.take(real_part.reshape(owned, -1), gmap, axis=1) * norm_factor  33.6 us
    unnamed x15, local copies, waits for them, and re-layouts  29 us
  transfers between devices with their start and end apart: 4, of which 3 were waited for; matrix products, arithmetic and copies ran while one was open for 5% of the time, Pallas kernels for 0%

commit v1 on v0

--- a/solution.py
+++ b/solution.py
@@ -88,7 +88,7 @@
         "ag,fgb->fab", left_wide[0], screened_rho[:, 1], precision=highest
     ) - jnp.einsum("ag,fgb->fab", left_wide[1], screened_rho[:, 0], precision=highest)
     partial_terms = jnp.stack([u_real, u_imag], axis=1) / math.sqrt(NG)
-    summed = lax.psum(partial_terms, ("row", "col"))
+    summed = lax.psum(lax.psum(partial_terms, "row"), "col")
     share_rows = NP // lax.axis_size(("row", "col"))
     return lax.dynamic_slice_in_dim(
         summed, lax.axis_index(("row", "col")) * share_rows, share_rows, 2

time: 696 us -> 728 us (1.046)
  waiting for transfers between devices: 253 us -> 285 us
    psum x1 -> x2, waiting for transfers between devices: 97.4 us -> 130 us  [shards(): summed = lax.psum(lax.psum(partial_terms, 'row'), 'col')]
  transfers between devices with their start and end apart: 4 -> 5, of which waited for: 3 -> 4; matrix products, arithmetic and copies ran while one was open for 5% -> 5% of each run, Pallas kernels for 0% -> 0%
where the time goes in v1:
time: 728 us; the launch traced here: 720 us
  waiting for transfers between devices  285 us (39%)
  local copies, waits for them, and re-layouts  251 us (34%)
  matrix products  112 us (15%)
  blocking collectives  40.2 us (6%)
  between operations  13.6 us (2%)
  other arithmetic  9.75 us (1%)
  starting transfers between devices  7.71 us (1%)
    psum x2, waiting for transfers between devices, shards(): summed = lax.psum(lax.psum(partial_terms, 'row'), 'col')  130 us
    all_gather x1, waiting for transfers between devices, shards(): lax.all_gather(halves, 'row', axis=1, tiled=True)  96.3 us
    all_to_all x1, waiting for transfers between devices, shards(): lax.all_to_all(density, ('row', 'col'), split_axis=0, concat_axis=1, tile...  59.1 us
    another operation x2, local copies, waits for them, and re-layouts, shards(): rho = jnp.stack([rho_real, rho_imag], axis=0).astype(jnp.bfloat16)  45.7 us
    all_to_all x1, blocking collectives, shards(): blocks = lax.all_to_all(rho, 'row', split_axis=2, concat_axis=1, tiled=True)  35.8 us
    gather x1, local copies, waits for them, and re-layouts, shards(): jnp.take(imag_part.reshape(owned, -1), gmap, axis=1) * norm_factor  33.6 us
    gather x1, local copies, waits for them, and re-layouts, shards(): jnp.take(real_part.reshape(owned, -1), gmap, axis=1) * norm_factor  33.6 us
    unnamed x15, local copies, waits for them, and re-layouts  29 us
  transfers between devices with their start and end apart: 5, of which 4 were waited for; matrix products, arithmetic and copies ran while one was open for 5% of the time, Pallas kernels for 0%

profile of v1, /device:TPU:0, one launch (start us, length us, event | category | flops | bytes accessed | tf_op | source)
XLA Modules:
  0.0 719.8 jit_solution(13501091259790191071)
XLA Ops:
  11.3 3.8 reshape.35
  15.1 7.5 %all-to-all-start = ((f32[384,2,1024]{2,1,0:T(2,128)}), f32[384,2,1024]{2,1,0:T(2,128)S(1)}, u32[]{:S(2)}, u32[]{:S(2)}) async-start(f32[384,2,1024]{2,1,0:T(2,128)} %reshape.35), calls=%async_computation | async-start | bytes 6291456 | tf_op jit(solution)/shard_map/all_to_all | solution.py:69
  22.7 59.1 %all-to-all-done = f32[384,2,1024]{2,1,0:T(2,128)S(1)} async-done(((f32[384,2,1024]{2,1,0:T(2,128)}), f32[384,2,1024]{2,1,0:T(2,128)S(1)}, u32[]{:S(2)}, u32[]{:S(2)}) %all-to-all-start) | async-done | bytes 3145760 | tf_op jit(solution)/shard_map/all_to_all | solution.py:69
  82.9 2.4 copy.71
  85.3 7.6 %reshape.36 = f32[768,32,32]{2,1,0:T(8,128)} reshape(f32[24,16,2,1024]{3,2,1,0:T(2,128)S(1)} %copy.71) | data formatting | bytes 6291456 | tf_op jit(solution)/shard_map/reshape | solution.py:23
  92.9 9.2 %copy.72 = f32[768,32,32]{0,2,1:T(8,128)S(1)} copy(f32[768,32,32]{2,1,0:T(8,128)} %reshape.36) | data formatting | bytes 6291456 | tf_op jit(solution)/shard_map/reshape | solution.py:23
  102.1 3.0 convolution_negate_fusion
  105.1 3.0 fusion.72
  108.1 4.9 fusion.22
  113.1 5.2 fusion.24
  118.2 6.7 add_bitcast_fusion.1
  125.0 5.5 subtract_bitcast_fusion.1
  130.5 10.6 %copy.79 = f32[768,32,32]{2,1,0:T(8,128)} copy(f32[768,32,32]{0,1,2:T(8,128)S(1)} %subtract_bitcast_fusion.1) | data formatting | bytes 6291456 | tf_op jit(solution)/shard_map/sub | solution.py:29
  141.1 9.4 %reshape.38 = f32[24,32,1024]{2,1,0:T(8,128)S(1)} reshape(f32[768,32,32]{2,1,0:T(8,128)} %copy.79) | data formatting | bytes 6291456 | tf_op jit(solution)/shard_map/reshape | solution.py:32
  150.4 5.5 fusion.66
  155.9 11.4 %copy.76 = f32[768,32,32]{2,1,0:T(8,128)} copy(f32[768,32,32]{0,1,2:T(8,128)} %add_bitcast_fusion.1) | data formatting | bytes 6291456 | tf_op jit(solution)/shard_map/add | solution.py:26
  167.3 10.7 %reshape.37 = f32[24,32,1024]{2,1,0:T(8,128)} reshape(f32[768,32,32]{2,1,0:T(8,128)} %copy.76) | data formatting | bytes 6291456 | tf_op jit(solution)/shard_map/reshape | solution.py:32
  178.0 5.9 fusion.69
  184.0 5.5 subtract_bitcast_fusion
  189.5 5.6 add_bitcast_fusion
  195.1 10.3 %copy.89 = f32[24,32,1024]{0,2,1:T(8,128)} copy(f32[24,32,1024]{2,1,0:T(8,128)} %add_bitcast_fusion) | data formatting | bytes 6291456 | tf_op jit(solution)/shard_map/reshape | solution.py:74
  205.4 8.6 %copy.90 = f32[24,32,1024]{0,2,1:T(8,128)} copy(f32[24,32,1024]{2,1,0:T(8,128)S(1)} %copy-done.2) | data formatting | bytes 6291456 | tf_op jit(solution)/shard_map/reshape | solution.py:75
  214.0 33.6 %gather_fusion = f32[8192,24]{1,0:T(8,128)} fusion(f32[24,32768]{0,1:T(8,128)} %bitcast.144, s32[8192]{0:T(1024)S(1)} %fusion.57), kind=kCustom, calls=%fused_computation.clone | custom fusion | bytes 1605632 | tf_op jit(solution)/shard_map/jit(_take)/gather | solution.py:74
  247.6 33.6 %gather_fusion.1 = f32[8192,24]{1,0:T(8,128)} fusion(f32[24,32768]{0,1:T(8,128)} %bitcast.143, s32[8192]{0:T(1024)S(1)} %fusion.57), kind=kCustom, calls=%fused_computation.1.clone | custom fusion | bytes 1605632 | tf_op jit(solution)/shard_map/jit(_take)/gather | solution.py:75
  281.3 7.2 fusion.30
  289.4 35.5 %copy.108 = bf16[2,24,8192]{1,0,2:T(2,128)(2,1)} copy(bf16[2,24,8192]{1,2,0:T(8,128)(2,1)S(1)} %pad_maximum_fusion) | data formatting | bytes 1572864 | tf_op jit(solution)/shard_map/stack | solution.py:76
  324.9 6.6 reshape.71
  331.5 35.8 %all_to_all.48 = bf16[8,2,24576]{2,1,0:T(2,128)(2,1)S(1)} all-to-all(bf16[8,2,24576]{2,1,0:T(2,128)(2,1)S(1)} %reshape.71), channel_id=1, replica_groups=mesh['kpt'=2,'row'=8,'col'=2] {'row'}, dimensions={0} | all-to-all | bytes 1572864 | tf_op jit(solution)/shard_map/all_to_all | solution.py:80
  367.3 6.9 reshape.72
  374.3 10.3 %copy.87 = bf16[2,24,8,1024]{3,1,2,0:T(8,128)(2,1)} copy(bf16[2,24,8,1024]{1,0,3,2:T(2,128)(2,1)} %bitcast.145) | data formatting | bytes 1572864 | tf_op jit(solution)/shard_map/all_to_all | solution.py:80
  384.6 10.2 %copy.109 = bf16[2,24,8192]{1,0,2:T(2,128)(2,1)} copy(bf16[2,24,8192]{1,2,0:T(8,128)(2,1)} %copy-done) | data formatting | bytes 1572864 | tf_op jit(solution)/shard_map/stack | solution.py:76
  394.8 7.0 reshape.73
  401.9 4.4 all_to_all.49
  406.2 7.3 %reshape.74 = bf16[8192,2,24]{2,1,0:T(2,128)(2,1)} reshape(bf16[2,2,98304]{2,1,0:T(2,128)(2,1)S(1)} %all_to_all.49) | data formatting | bytes 1572864
  413.6 9.5 %copy.83 = bf16[2,24,2,4096]{3,1,2,0:T(8,128)(2,1)} copy(bf16[2,24,2,4096]{1,0,3,2:T(2,128)(2,1)} %bitcast.146) | data formatting | bytes 1572864 | tf_op jit(solution)/shard_map/all_to_all | solution.py:78
  424.7 96.3 %all-gather.3.cloned.1.call-done = bf16[2,384,4096]{2,1,0:T(8,128)(2,1)} async-done(((bf16[2,48,4096]{2,1,0:T(8,128)(2,1)}), bf16[2,384,4096]{2,1,0:T(8,128)(2,1)}) %all-gather.3.cloned.1.call-update) | async-done | bytes 6291472 | tf_op jit(solution)/shard_map/all_gather | solution.py:79
  521.0 11.4 %fusion = f32[384,2,1024]{2,0,1:T(8,128)S(1)} fusion(bf16[2,2,1024,4096]{3,2,1,0:T(8,128)(2,1)} %param.9, bf16[2,384,4096]{2,1,0:T(8,128)(2,1)} %all-gather.3.cloned.1.call-done), kind=kOutput, calls=%fused_computation.2 | convolution fusion | flops 6442450944 | bytes 23068672 | tf_op jit(solution)/shard_map/fgh,bh->fgb/dot_general | solution.py:53
  532.3 11.2 %fusion.39 = f32[384,2,1024]{2,0,1:T(8,128)S(1)} fusion(f32[384,2,1024]{2,0,1:T(8,128)S(1)} %fusion, bf16[2,2,1024,4096]{3,2,1,0:T(8,128)(2,1)} %param.9, bf16[2,384,4096]{2,1,0:T(8,128)(2,1)} %all-gather.3.cloned.1.call-done), kind=kOutput, calls=%fused_computation.47 | convolution fusion | flops 6443237376 | bytes 26214400 | tf_op jit(solution)/shard_map/fgh,bh->fgb/dot_general | solution.py:52
  543.6 2.6 fusion.14
  546.2 2.6 fusion.16
  548.9 12.6 %fusion.2 = f32[384,2,1024]{2,0,1:T(8,128)} fusion(bf16[2,2,1024,4096]{3,2,1,0:T(8,128)(2,1)} %param.9, bf16[2,384,4096]{2,1,0:T(8,128)(2,1)} %all-gather.3.cloned.1.call-done), kind=kOutput, calls=%fused_computation.4 | convolution fusion | flops 6442450944 | bytes 23068672 | tf_op jit(solution)/shard_map/fgh,bh->fgb/dot_general | solution.py:51
  561.5 11.9 %fusion.36 = f32[384,2,1024]{2,0,1:T(8,128)S(1)} fusion(f32[384,2,1024]{2,0,1:T(8,128)} %fusion.2, bf16[2,2,1024,4096]{3,2,1,0:T(8,128)(2,1)} %param.9, bf16[2,384,4096]{2,1,0:T(8,128)(2,1)} %all-gather.3.cloned.1.call-done), kind=kOutput, calls=%fused_computation.46 | convolution fusion | flops 6443237376 | bytes 26214400 | tf_op jit(solution)/shard_map/fgh,bh->fgb/dot_general | solution.py:50
  573.3 2.7 fusion.48
  576.0 2.7 fusion.51
  578.7 1.6 maximum_multiply_fusion
  580.4 106.9 %all-reduce.3.cloned.1.call-done = f32[2,2,384,384]{2,3,0,1:T(8,128)} async-done(((f32[2,2,384,384]{2,3,0,1:T(8,128)}), f32[2,2,384,384]{2,3,0,1:T(8,128)}) %all-reduce.3.cloned.1.call-update) | async-done | bytes 2359312 | tf_op jit(solution)/shard_map/psum | solution.py:91
  687.3 23.1 %all-reduce.5.cloned.1.call-done = f32[2,2,384,384]{2,3,0,1:T(8,128)} async-done(((f32[2,2,384,384]{2,3,0,1:T(8,128)}), f32[2,2,384,384]{2,3,0,1:T(8,128)}) %all-reduce.5.cloned.1.call-update) | async-done | bytes 2359312 | tf_op jit(solution)/shard_map/psum | solution.py:91
  710.4 1.7 constant_dynamic-slice_fusion
  (29 shorter events, 9.5 us)
Async XLA Ops:
  15.1 7.6 %copy-start.4 = (s32[8192]{0:T(1024)S(1)}, s32[8192]{0:T(1024)}, u32[]{:S(2)}) copy-start(s32[8192]{0:T(1024)} %param.8) | copy-start | bytes 98308
  15.1 66.8 %all-to-all-start = ((f32[384,2,1024]{2,1,0:T(2,128)}), f32[384,2,1024]{2,1,0:T(2,128)S(1)}, u32[]{:S(2)}, u32[]{:S(2)}) async-start(f32[384,2,1024]{2,1,0:T(2,128)} %reshape.35), calls=%async_computation | async-start | bytes 6291456 | tf_op jit(solution)/shard_map/all_to_all | solution.py:69
  22.6 400.5 %all-gather.5.cloned.1.call-start = ((), (), s32[]{:S(2)}) async-start(), calls=%async_computation.4 | async-start | bytes 2359296 | tf_op jit(solution)/shard_map/all_gather | solution.py:82
  178.0 6.0 copy-start.1
  178.0 6.0 copy-start.3
  195.1 10.3 %copy-start.2 = (f32[24,32,1024]{2,1,0:T(8,128)S(1)}, f32[24,32,1024]{2,1,0:T(8,128)}, u32[]{:S(2)}) copy-start(f32[24,32,1024]{2,1,0:T(8,128)} %subtract_bitcast_fusion) | copy-start | bytes 9437188
  289.4 35.5 %copy-start = (bf16[2,24,8192]{1,2,0:T(8,128)(2,1)}, bf16[2,24,8192]{1,2,0:T(8,128)(2,1)S(1)}, u32[]{:S(2)}) copy-start(bf16[2,24,8192]{1,2,0:T(8,128)(2,1)S(1)} %pad_maximum_fusion) | copy-start | bytes 2359300
  384.6 136.4 %all-gather.3.cloned.1.call-start = ((), (), s32[]{:S(2)}) async-start(), calls=%async_computation.3 | async-start | bytes 7077888 | tf_op jit(solution)/shard_map/all_gather | solution.py:79
  423.1 264.2 %all-reduce.3.cloned.1.call-start = ((), (), s32[]{:S(2)}) async-start(), calls=%async_computation.5 | async-start | bytes 4718592 | tf_op jit(solution)/shard_map/psum | solution.py:91
  580.3 130.1 %all-reduce.5.cloned.1.call-start = ((), (), s32[]{:S(2)}) async-start(), calls=%async_computation.6 | async-start | bytes 4718592 | tf_op jit(solution)/shard_map/psum | solution.py:91
Sparse Core Ops, SparseCore 0:
  384.7 8.8 all-gather.4
  423.2 97.7 all-gather.2
  580.5 106.7 all-reduce.2
  689.5 20.9 all-reduce.4
